TPU v7x, 256 devices: a whole 4x4x8 slice. The times are simulated.
256 devices in a mesh: dp: 16 (over y, x_hi, core), tensor: 16 (over x_lo, z).
Axes of the slice: x: 4 (x_hi: 2, x_lo: 2; x = x_hi * 2 + x_lo), y: 4, z: 8, core: 2. Of those that a mesh axis runs over, the one named last changes fastest.
Arguments:
- h_values: bfloat16 [12288, 16384], P(('dp', 'tensor')), may hold values from -448 to 448
- h_scales: bfloat16 [12288, 128], P(('dp', 'tensor')), may hold values from 0.00049972534 to 0.0099487305
- dy_values: bfloat16 [12288, 4096], P(('dp', 'tensor')), may hold values from -448 to 448
- dy_scales: bfloat16 [12288, 32], P(('dp', 'tensor')), may hold values from 1.9907951e-05 to 0.00039863586
Outputs:
- grad_down: bfloat16 [4096, 16384], P('dp', 'tensor')
All inputs are finite; a program needn't handle non-finite values.
Results may differ from a plain program's by a relative error of at most 0.02.
Values may be sent and summed in bfloat16 or wider, within the bound.
A program may use at most 192 MiB of HBM per device.

v0:
```python
import jax
import jax.numpy as jnp
from jax import lax
from jax.sharding import PartitionSpec as P

QBLOCK = 128


def dequantize(values, scales):
    row_count, col_count = values.shape
    block_total = scales.shape[1]
    widened = values.astype(jnp.float32).reshape(row_count, block_total, col_count // block_total)
    widened = widened * scales.astype(jnp.float32)[:, :, None]
    return widened.reshape(row_count, col_count)


def requantize(field):
    row_count, col_count = field.shape
    blocked = field.reshape(row_count // QBLOCK, QBLOCK, col_count)
    largest = jnp.max(jnp.abs(blocked), axis=1)
    column_scale = ((largest + 1e-06) / 448.0).astype(jnp.bfloat16)
    quantized = (blocked / column_scale.astype(jnp.float32)[:, None, :]).astype(jnp.bfloat16)
    return (quantized.reshape(row_count, col_count), column_scale)


def group_product(grad_q, grad_scale, hidden_q, hidden_scale):
    block_count = grad_q.shape[0] // QBLOCK
    summed = jnp.zeros((grad_q.shape[1], hidden_q.shape[1]), jnp.float32)
    for block_index in range(block_count):
        grad_block = grad_q[block_index * QBLOCK : (block_index + 1) * QBLOCK]
        hidden_block = hidden_q[block_index * QBLOCK : (block_index + 1) * QBLOCK]
        product = lax.dot_general(
            grad_block, hidden_block, (((0,), (0,)), ((), ())), preferred_element_type=jnp.float32
        )
        row_factor = grad_scale[block_index].astype(jnp.float32)[:, None]
        col_factor = hidden_scale[block_index].astype(jnp.float32)[None, :]
        summed = summed + product * row_factor * col_factor
    return summed


def shards(h_values, h_scales, dy_values, dy_scales):
    hidden_vals, hidden_blocks = (
        lax.all_to_all(h_values, "tensor", split_axis=1, concat_axis=0, tiled=True),
        lax.all_to_all(h_scales, "tensor", split_axis=1, concat_axis=0, tiled=True),
    )
    grad_vals, grad_blocks = (
        lax.all_gather(dy_values, "tensor", axis=0, tiled=True),
        lax.all_gather(dy_scales, "tensor", axis=0, tiled=True),
    )
    hidden_q, hidden_scale = requantize(dequantize(hidden_vals, hidden_blocks))
    grad_q, grad_scale = requantize(dequantize(grad_vals, grad_blocks))
    return lax.psum_scatter(
        group_product(grad_q, grad_scale, hidden_q, hidden_scale).astype(jnp.bfloat16),
        "dp",
        scatter_dimension=0,
        tiled=True,
    )


def solution(mesh):
    placed = (
        P(("dp", "tensor"), None),
        P(("dp", "tensor"), None),
        P(("dp", "tensor"), None),
        P(("dp", "tensor"), None),
    )
    return jax.shard_map(
        shards, mesh=mesh, in_specs=placed, out_specs=P("dp", "tensor"), check_vma=False
    )
```

profile of v0, /device:TPU:8, one launch (start us, length us, event | category | flops | bytes accessed | tf_op | source)
XLA Modules:
  0.0 344.4 jit_solution(2101893840816630577)
XLA Ops:
  6.5 0.0 all-gather.3.cloned.1.call-start
  6.5 0.7 all-gather.3.cloned.1.call-update
  7.3 0.8 copy.19
  8.1 0.7 reshape.117
  8.8 9.5 %all-to-all-start.1 = ((bf16[16,2,192]{2,1,0:T(2,128)(2,1)}), bf16[16,2,192]{2,1,0:T(2,128)(2,1)S(1)}, u32[]{:S(2)}, u32[]{:S(2)}) async-start(bf16[16,2,192]{2,1,0:T(2,128)(2,1)} %reshape.117), calls=%async_computation.1 | async-start | bytes 32768 | tf_op jit(solution)/shard_map/all_to_all | solution.py:44
  18.3 2.7 copy.28
  21.0 5.8 %all-to-all-done.1 = bf16[16,2,192]{2,1,0:T(2,128)(2,1)S(1)} async-done(((bf16[16,2,192]{2,1,0:T(2,128)(2,1)}), bf16[16,2,192]{2,1,0:T(2,128)(2,1)S(1)}, u32[]{:S(2)}, u32[]{:S(2)}) %all-to-all-start.1) | async-done | bytes 12320 | tf_op jit(solution)/shard_map/all_to_all | solution.py:44
  26.8 4.4 %all-to-all-start = ((bf16[48,16,1024]{2,0,1:T(8,128)(2,1)}), bf16[48,16,1024]{2,0,1:T(8,128)(2,1)}, u32[]{:S(2)}, u32[]{:S(2)}) async-start(bf16[48,16,1024]{2,0,1:T(8,128)(2,1)} %bitcast.67), calls=%async_computation | async-start | bytes 3145728 | tf_op jit(solution)/shard_map/all_to_all | solution.py:43
  31.2 0.0 reduce-scatter.2.cloned.1.call-start
  31.3 82.0 %all-gather = bf16[16,48,32]{1,2,0:T(8,128)(2,1)S(1)} all-gather(bf16[1,48,32]{1,2,0:T(8,128)(2,1)} %bitcast.80), channel_id=1, replica_groups=mesh['dp'=16,'tensor'=16] {'tensor'}, dimensions={0}, use_global_device_ids=true | all-gather | bytes 52224 | tf_op jit(solution)/shard_map/all_gather | solution.py:48
  113.3 0.1 copy.22
  113.4 7.1 %mul.148 = f32[768,32,128]{2,1,0:T(8,128)} broadcast(f32[768,32]{1,0:T(8,128)S(1)} %bitcast.71), dimensions={0,1} | broadcast | bytes 12681216 | tf_op jit(solution)/shard_map/mul | solution.py:13
  120.5 13.8 %mul.149 = f32[6,128,4096]{2,1,0:T(8,128)} reshape(f32[768,32,128]{2,1,0:T(8,128)} %mul.148) | data formatting | bytes 25165824 | tf_op jit(solution)/shard_map/mul | solution.py:13
  134.3 0.1 reshape.118
  134.4 0.2 copy.23
  134.6 0.9 mul.151
  135.4 2.4 mul.152
  137.8 0.0 all-to-all-done
  137.8 1.8 convert_element_type.171
  139.6 2.6 abs_reduce_fusion.1
  142.3 0.5 divide_convert_fusion.1
  142.8 0.0 all-gather.3.cloned.1.call-done
  142.8 8.5 %abs_reduce_fusion = f32[6,4096]{1,0:T(8,128)S(1)} fusion(f32[6,128,4096]{2,1,0:T(8,128)} %mul.149, bf16[6,128,4096]{2,1,0:T(8,128)(2,1)} %bitcast.68), kind=kLoop, calls=%fused_computation.3 | loop fusion | flops 12558336 | bytes 18972672 | tf_op jit(solution)/shard_map/reduce_max | solution.py:20
  151.3 7.6 %divide_convert_fusion = bf16[6,128,4096]{2,1,0:T(8,128)(2,1)S(1)} fusion(f32[6,128,4096]{2,1,0:T(8,128)} %mul.149, bf16[6,128,4096]{2,1,0:T(8,128)(2,1)} %bitcast.69, f32[6,4096]{1,0:T(8,128)S(1)} %get-tuple-element.9), kind=kLoop, calls=%fused_computation.2 | loop fusion | flops 12582912 | bytes 25264128 | tf_op jit(solution)/shard_map/convert_element_type | solution.py:22
  158.9 0.0 copy-start
  158.9 8.1 %fusion = f32[4096,1024]{1,0:T(8,128)} fusion(bf16[6,128,4096]{2,1,0:T(8,128)(2,1)S(1)} %divide_convert_fusion, bf16[6,128,1024]{2,1,0:T(8,128)(2,1)S(1)} %divide_convert_fusion.1), kind=kOutput, calls=%fused_computation.9 | convolution fusion | flops 1073741824 | bytes 18087936 | tf_op jit(solution)/shard_map/dot_general | solution.py:32
  167.0 8.1 %fusion.1 = f32[4096,1024]{1,0:T(8,128)} fusion(bf16[6,128,4096]{2,1,0:T(8,128)(2,1)S(1)} %divide_convert_fusion, bf16[6,128,1024]{2,1,0:T(8,128)(2,1)S(1)} %divide_convert_fusion.1), kind=kOutput, calls=%fused_computation.11 | convolution fusion | flops 1073741824 | bytes 18087936 | tf_op jit(solution)/shard_map/dot_general | solution.py:32
  175.1 8.1 %fusion.2 = f32[4096,1024]{1,0:T(8,128)} fusion(bf16[6,128,4096]{2,1,0:T(8,128)(2,1)S(1)} %divide_convert_fusion, bf16[6,128,1024]{2,1,0:T(8,128)(2,1)S(1)} %divide_convert_fusion.1), kind=kOutput, calls=%fused_computation.13 | convolution fusion | flops 1073741824 | bytes 18087936 | tf_op jit(solution)/shard_map/dot_general | solution.py:32
  183.2 8.1 %fusion.3 = f32[4096,1024]{1,0:T(8,128)} fusion(bf16[6,128,4096]{2,1,0:T(8,128)(2,1)S(1)} %divide_convert_fusion, bf16[6,128,1024]{2,1,0:T(8,128)(2,1)S(1)} %divide_convert_fusion.1), kind=kOutput, calls=%fused_computation.15 | convolution fusion | flops 1073741824 | bytes 18087936 | tf_op jit(solution)/shard_map/dot_general | solution.py:32
  191.3 0.0 copy-done
  191.3 8.2 %fusion.4 = f32[4096,1024]{1,0:T(8,128)} fusion(bf16[6,128,4096]{2,1,0:T(8,128)(2,1)S(1)} %divide_convert_fusion, bf16[6,128,1024]{2,1,0:T(8,128)(2,1)S(1)} %divide_convert_fusion.1), kind=kOutput, calls=%fused_computation.17 | convolution fusion | flops 1073741824 | bytes 18087936 | tf_op jit(solution)/shard_map/dot_general | solution.py:32
  199.5 0.1 slice_convert_fusion.5
  199.6 32.2 %add_convert_fusion = bf16[4096,1024]{1,0:T(8,128)(2,1)} fusion(f32[4096,1024]{1,0:T(8,128)} %fusion, f32[4096,1024]{1,0:T(8,128)} %fusion.1, f32[4096,1024]{1,0:T(8,128)} %fusion.2, f32[4096,1024]{1,0:T(8,128)} %fusion.3, f32[4096,1024]{1,0:T(8,128)} %fusion.4, f32[1024]{0:T(1024)S(1)} %bitcast.86, f32[4096]{0:T(1024)S(1)} %bitcast.79, ...), kind=kOutput, calls=%fused_computation | convolution fusion | flops 1149239296 | bytes 93708288 | tf_op jit(solution)/shard_map/dot_general | solution.py:32
  231.8 0.0 reduce-scatter.2.cloned.1.call-update
  231.8 105.8 %reduce-scatter.2.cloned.1.call-done = bf16[256,1024]{1,0:T(8,128)(2,1)} async-done(((bf16[4096,1024]{1,0:T(8,128)(2,1)}), bf16[256,1024]{1,0:T(8,128)(2,1)}) %reduce-scatter.2.cloned.1.call-update) | async-done | bytes 524304 | tf_op jit(solution)/shard_map/reduce_scatter | solution.py:52
  (5 shorter events, 0.1 us)
Async XLA Ops:
  6.5 136.3 %all-gather.3.cloned.1.call-start = ((), (), s32[]{:S(2)}) async-start(), calls=%async_computation.3 | async-start | bytes 6684672 | tf_op jit(solution)/shard_map/all_gather | solution.py:47
  8.8 18.0 %all-to-all-start.1 = ((bf16[16,2,192]{2,1,0:T(2,128)(2,1)}), bf16[16,2,192]{2,1,0:T(2,128)(2,1)S(1)}, u32[]{:S(2)}, u32[]{:S(2)}) async-start(bf16[16,2,192]{2,1,0:T(2,128)(2,1)} %reshape.117), calls=%async_computation.1 | async-start | bytes 32768 | tf_op jit(solution)/shard_map/all_to_all | solution.py:44
  26.8 111.0 %all-to-all-start = ((bf16[48,16,1024]{2,0,1:T(8,128)(2,1)}), bf16[48,16,1024]{2,0,1:T(8,128)(2,1)}, u32[]{:S(2)}, u32[]{:S(2)}) async-start(bf16[48,16,1024]{2,0,1:T(8,128)(2,1)} %bitcast.67), calls=%async_computation | async-start | bytes 3145728 | tf_op jit(solution)/shard_map/all_to_all | solution.py:43
  31.2 306.4 %reduce-scatter.2.cloned.1.call-start = ((), (), s32[]{:S(2)}) async-start(), calls=%async_computation.4 | async-start | bytes 8912896 | tf_op jit(solution)/shard_map/reduce_scatter | solution.py:52
  158.9 32.4 %copy-start = (bf16[6,128,4096]{2,1,0:T(8,128)(2,1)}, bf16[6,128,4096]{2,1,0:T(8,128)(2,1)S(1)}, u32[]{:S(2)}) copy-start(bf16[6,128,4096]{2,1,0:T(8,128)(2,1)S(1)} %divide_convert_fusion) | copy-start | bytes 18874372
Sparse Core Ops, SparseCore 0:
  9.1 119.8 all-gather.2
  231.9 105.6 reduce-scatter.1
where the time goes:
time: 345 us; the launch traced here: 344 us
  waiting for transfers between devices  112 us (32%)
  blocking collectives  82 us (24%)
  matrix products  72.7 us (21%)
  local copies, waits for them, and re-layouts  28.8 us (8%)
  other arithmetic  21.1 us (6%)
  starting transfers between devices  13.9 us (4%)
  between operations  13.5 us (4%)
    reduce_scatter x1, waiting for transfers between devices, shards(): lax.psum_scatter(group_product(grad_q, grad_scale, hidden_q, hidden_scale...  106 us
    all_gather x1, blocking collectives, shards(): lax.all_gather(dy_scales, 'tensor', axis=0, tiled=True)  82 us
    dot_general x6, matrix products, group_product(): lax.dot_general(grad_block, hidden_block, (((0,), (0,)), ((), ())), prefe...  72.7 us
    mul x4, local copies, waits for them, and re-layouts, dequantize(): widened = widened * scales.astype(jnp.float32)[:, :, None]  24.1 us
    reduce_max x2, other arithmetic, requantize(): largest = jnp.max(jnp.abs(blocked), axis=1)  11.1 us
    all_to_all x1, starting transfers between devices, shards(): lax.all_to_all(h_scales, 'tensor', split_axis=1, concat_axis=0, tiled=True)  9.5 us
    convert_element_type x2, other arithmetic, requantize(): (blocked / column_scale.astype(jnp.float32)[:, None, :]).astype(jnp.bfloa...  8.04 us
  transfers between devices with their start and end apart: 4, of which 2 were waited for; matrix products, arithmetic and copies ran while one was open for 10% of the time, Pallas kernels for 0%

commit v1 on v0

--- a/solution.py
+++ b/solution.py
@@ -45,7 +45,9 @@
     )
     grad_vals, grad_blocks = (
         lax.all_gather(dy_values, "tensor", axis=0, tiled=True),
-        lax.all_gather(dy_scales, "tensor", axis=0, tiled=True),
+        jnp.concatenate(
+            lax.all_to_all(jnp.stack([dy_scales] * lax.axis_size("tensor")), "tensor", 0, 0), axis=0
+        ),
     )
     hidden_q, hidden_scale = requantize(dequantize(hidden_vals, hidden_blocks))
     grad_q, grad_scale = requantize(dequantize(grad_vals, grad_blocks))

time: 345 us -> 332 us (0.962)
  blocking collectives: 82 us -> 0 us
  waiting for transfers between devices: 112 us -> 178 us
  starting transfers between devices: 13.9 us -> 17.4 us
    all_gather x1 -> x0, blocking collectives: 82 us -> none  [shards(): lax.all_gather(dy_scales, 'tensor', axis=0, tiled=True)]
    all_to_all x1, waiting for transfers between devices: 0.01 us -> 29.7 us  [shards(): lax.all_to_all(h_values, 'tensor', split_axis=1, concat_axis=0, tiled=True)]
    all_gather x1, waiting for transfers between devices: 0.02 us -> 27.2 us  [shards(): lax.all_gather(dy_values, 'tensor', axis=0, tiled=True)]
    all_to_all x0 -> x1, waiting for transfers between devices: none -> 5.89 us  [shards(): lax.all_to_all(jnp.stack([dy_scales] * lax.axis_size('tensor')), 'tensor'...]
    all_to_all x0 -> x1, starting transfers between devices: none -> 3.5 us  [shards(): lax.all_to_all(jnp.stack([dy_scales] * lax.axis_size('tensor')), 'tensor'...]
  transfers between devices with their start and end apart: 4 -> 5, of which waited for: 2 -> 5; matrix products, arithmetic and copies ran while one was open for 10% -> 10% of each run, Pallas kernels for 0% -> 0%
where the time goes in v1:
time: 332 us
  waiting for transfers between devices  178 us (54%)
  matrix products  72.8 us (22%)
  local copies, waits for them, and re-layouts  30.8 us (9%)
  other arithmetic  19.2 us (6%)
  starting transfers between devices  17.4 us (5%)
  between operations  13.6 us (4%)
    reduce_scatter x1, waiting for transfers between devices, shards(): lax.psum_scatter(group_product(grad_q, grad_scale, hidden_q, hidden_scale...  107 us
    dot_general x6, matrix products, group_product(): lax.dot_general(grad_block, hidden_block, (((0,), (0,)), ((), ())), prefe...  72.8 us
    all_to_all x1, waiting for transfers between devices, shards(): lax.all_to_all(h_values, 'tensor', split_axis=1, concat_axis=0, tiled=True)  29.7 us
    all_gather x1, waiting for transfers between devices, shards(): lax.all_gather(dy_values, 'tensor', axis=0, tiled=True)  27.2 us
    mul x4, local copies, waits for them, and re-layouts, dequantize(): widened = widened * scales.astype(jnp.float32)[:, :, None]  24.2 us
    all_to_all x1, starting transfers between devices, shards(): lax.all_to_all(h_scales, 'tensor', split_axis=1, concat_axis=0, tiled=True)  9.5 us
    reduce_max x2, other arithmetic, requantize(): largest = jnp.max(jnp.abs(blocked), axis=1)  9.24 us
    convert_element_type x2, other arithmetic, requantize(): (blocked / column_scale.astype(jnp.float32)[:, None, :]).astype(jnp.bfloa...  8.04 us
  transfers between devices with their start and end apart: 5, of which 5 were waited for; matrix products, arithmetic and copies ran while one was open for 10% of the time, Pallas kernels for 0%

profile of v1, /device:TPU:8, one launch (start us, length us, event | category | flops | bytes accessed | tf_op | source)
XLA Modules:
  0.0 331.6 jit_solution(15474981177428751049)
XLA Ops:
  6.5 0.0 copy-start
  6.5 0.0 all-gather.2.cloned.1.call-start
  6.5 0.7 all-gather.2.cloned.1.call-update
  7.3 0.8 copy.22
  8.1 0.7 reshape.126
  8.8 9.5 %all-to-all-start.2 = ((bf16[16,2,192]{2,1,0:T(2,128)(2,1)}), bf16[16,2,192]{2,1,0:T(2,128)(2,1)S(1)}, u32[]{:S(2)}, u32[]{:S(2)}) async-start(bf16[16,2,192]{2,1,0:T(2,128)(2,1)} %reshape.126), calls=%async_computation.2 | async-start | bytes 32768 | tf_op jit(solution)/shard_map/all_to_all | solution.py:44
  18.3 0.0 copy-done
  18.3 0.8 reshape.124
  19.2 7.6 %all-to-all-done.2 = bf16[16,2,192]{2,1,0:T(2,128)(2,1)S(1)} async-done(((bf16[16,2,192]{2,1,0:T(2,128)(2,1)}), bf16[16,2,192]{2,1,0:T(2,128)(2,1)S(1)}, u32[]{:S(2)}, u32[]{:S(2)}) %all-to-all-start.2) | async-done | bytes 12320 | tf_op jit(solution)/shard_map/all_to_all | solution.py:44
  26.8 3.5 %all-to-all-start = ((bf16[16,2,768]{2,1,0:T(2,128)(2,1)}), bf16[16,2,768]{2,1,0:T(2,128)(2,1)S(1)}, u32[]{:S(2)}, u32[]{:S(2)}) async-start(bf16[16,2,768]{2,1,0:T(2,128)(2,1)} %reshape.124), calls=%async_computation | async-start | bytes 98304 | tf_op jit(solution)/shard_map/all_to_all | solution.py:49
  30.3 2.8 copy.31
  33.1 5.9 %all-to-all-done = bf16[16,2,768]{2,1,0:T(2,128)(2,1)S(1)} async-done(((bf16[16,2,768]{2,1,0:T(2,128)(2,1)}), bf16[16,2,768]{2,1,0:T(2,128)(2,1)S(1)}, u32[]{:S(2)}, u32[]{:S(2)}) %all-to-all-start) | async-done | bytes 49184 | tf_op jit(solution)/shard_map/all_to_all | solution.py:49
  39.0 0.0 copy-start.4
  39.0 4.4 %all-to-all-start.1 = ((bf16[48,16,1024]{2,0,1:T(8,128)(2,1)}), bf16[48,16,1024]{2,0,1:T(8,128)(2,1)}, u32[]{:S(2)}, u32[]{:S(2)}) async-start(bf16[48,16,1024]{2,0,1:T(8,128)(2,1)} %bitcast.69), calls=%async_computation.1 | async-start | bytes 3145728 | tf_op jit(solution)/shard_map/all_to_all | solution.py:43
  43.4 0.0 reduce-scatter.2.cloned.1.call-start
  43.4 0.0 copy-done.4
  43.5 0.1 reshape.127
  43.6 0.2 copy.26
  43.7 0.9 mul.151
  44.6 2.3 mul.152
  46.9 1.0 reshape.125
  47.9 0.1 copy.25
  48.0 7.0 %mul.148 = f32[768,32,128]{2,1,0:T(8,128)} broadcast(f32[768,32]{1,0:T(8,128)S(1)} %bitcast.73), dimensions={0,1} | broadcast | bytes 12681216 | tf_op jit(solution)/shard_map/mul | solution.py:13
  55.1 0.0 copy-start.3
  55.1 14.0 %mul.149 = f32[6,128,4096]{2,1,0:T(8,128)} reshape(f32[768,32,128]{2,1,0:T(8,128)} %mul.148) | data formatting | bytes 25165824 | tf_op jit(solution)/shard_map/mul | solution.py:13
  69.1 29.7 %all-to-all-done.1 = bf16[48,16,1024]{2,0,1:T(8,128)(2,1)} async-done(((bf16[48,16,1024]{2,0,1:T(8,128)(2,1)}), bf16[48,16,1024]{2,0,1:T(8,128)(2,1)}, u32[]{:S(2)}, u32[]{:S(2)}) %all-to-all-start.1) | async-done | bytes 1572896 | tf_op jit(solution)/shard_map/all_to_all | solution.py:43
  98.8 1.8 convert_element_type.180
  100.6 0.0 copy-done.3
  100.6 0.8 abs_reduce_fusion.1
  101.4 0.4 divide_convert_fusion.1
  101.9 27.2 %all-gather.2.cloned.1.call-done = bf16[768,4096]{1,0:T(8,128)(2,1)} async-done(((bf16[48,4096]{1,0:T(8,128)(2,1)}), bf16[768,4096]{1,0:T(8,128)(2,1)}) %all-gather.2.cloned.1.call-update) | async-done | bytes 6291472 | tf_op jit(solution)/shard_map/all_gather | solution.py:47
  129.1 8.5 %abs_reduce_fusion = f32[6,4096]{1,0:T(8,128)S(1)} fusion(f32[6,128,4096]{2,1,0:T(8,128)} %mul.149, bf16[6,128,4096]{2,1,0:T(8,128)(2,1)} %bitcast.70), kind=kLoop, calls=%fused_computation.3 | loop fusion | flops 12558336 | bytes 18972672 | tf_op jit(solution)/shard_map/reduce_max | solution.py:20
  137.7 7.6 %divide_convert_fusion = bf16[6,128,4096]{2,1,0:T(8,128)(2,1)S(1)} fusion(f32[6,128,4096]{2,1,0:T(8,128)} %mul.149, bf16[6,128,4096]{2,1,0:T(8,128)(2,1)} %bitcast.71, f32[6,4096]{1,0:T(8,128)S(1)} %get-tuple-element.9), kind=kLoop, calls=%fused_computation.2 | loop fusion | flops 12582912 | bytes 25264128 | tf_op jit(solution)/shard_map/convert_element_type | solution.py:22
  145.2 0.0 copy-start.2
  145.3 8.1 %fusion = f32[4096,1024]{1,0:T(8,128)} fusion(bf16[6,128,4096]{2,1,0:T(8,128)(2,1)S(1)} %divide_convert_fusion, bf16[6,128,1024]{2,1,0:T(8,128)(2,1)S(1)} %divide_convert_fusion.1), kind=kOutput, calls=%fused_computation.9 | convolution fusion | flops 1073741824 | bytes 18087936 | tf_op jit(solution)/shard_map/dot_general | solution.py:32
  153.4 8.1 %fusion.1 = f32[4096,1024]{1,0:T(8,128)} fusion(bf16[6,128,4096]{2,1,0:T(8,128)(2,1)S(1)} %divide_convert_fusion, bf16[6,128,1024]{2,1,0:T(8,128)(2,1)S(1)} %divide_convert_fusion.1), kind=kOutput, calls=%fused_computation.11 | convolution fusion | flops 1073741824 | bytes 18087936 | tf_op jit(solution)/shard_map/dot_general | solution.py:32
  161.5 8.1 %fusion.2 = f32[4096,1024]{1,0:T(8,128)} fusion(bf16[6,128,4096]{2,1,0:T(8,128)(2,1)S(1)} %divide_convert_fusion, bf16[6,128,1024]{2,1,0:T(8,128)(2,1)S(1)} %divide_convert_fusion.1), kind=kOutput, calls=%fused_computation.13 | convolution fusion | flops 1073741824 | bytes 18087936 | tf_op jit(solution)/shard_map/dot_general | solution.py:32
  169.6 8.1 %fusion.3 = f32[4096,1024]{1,0:T(8,128)} fusion(bf16[6,128,4096]{2,1,0:T(8,128)(2,1)S(1)} %divide_convert_fusion, bf16[6,128,1024]{2,1,0:T(8,128)(2,1)S(1)} %divide_convert_fusion.1), kind=kOutput, calls=%fused_computation.15 | convolution fusion | flops 1073741824 | bytes 18087936 | tf_op jit(solution)/shard_map/dot_general | solution.py:32
  177.7 0.0 copy-done.2
  177.7 8.2 %fusion.4 = f32[4096,1024]{1,0:T(8,128)} fusion(bf16[6,128,4096]{2,1,0:T(8,128)(2,1)S(1)} %divide_convert_fusion, bf16[6,128,1024]{2,1,0:T(8,128)(2,1)S(1)} %divide_convert_fusion.1), kind=kOutput, calls=%fused_computation.17 | convolution fusion | flops 1073741824 | bytes 18087936 | tf_op jit(solution)/shard_map/dot_general | solution.py:32
  185.8 0.1 slice_convert_fusion.5
  185.9 0.0 copy-start.1
  185.9 32.2 %add_convert_fusion = bf16[4096,1024]{1,0:T(8,128)(2,1)} fusion(f32[4096,1024]{1,0:T(8,128)} %fusion, f32[4096,1024]{1,0:T(8,128)} %fusion.1, f32[4096,1024]{1,0:T(8,128)} %fusion.2, f32[4096,1024]{1,0:T(8,128)} %fusion.3, f32[4096,1024]{1,0:T(8,128)} %fusion.4, f32[1024]{0:T(1024)S(1)} %bitcast.88, f32[4096]{0:T(1024)S(1)} %bitcast.82, ...), kind=kOutput, calls=%fused_computation | convolution fusion | flops 1149239296 | bytes 93708288 | tf_op jit(solution)/shard_map/dot_general | solution.py:32
  218.2 0.0 reduce-scatter.2.cloned.1.call-update
  218.2 106.6 %reduce-scatter.2.cloned.1.call-done = bf16[256,1024]{1,0:T(8,128)(2,1)} async-done(((bf16[4096,1024]{1,0:T(8,128)(2,1)}), bf16[256,1024]{1,0:T(8,128)(2,1)}) %reduce-scatter.2.cloned.1.call-update) | async-done | bytes 524304 | tf_op jit(solution)/shard_map/reduce_scatter | solution.py:54
  324.8 0.0 copy-done.1
  (6 shorter events, 0.1 us)
Async XLA Ops:
  6.5 11.8 %copy-start = (bf16[48,32]{0,1:T(8,128)(2,1)S(1)}, bf16[48,32]{0,1:T(8,128)(2,1)}, u32[]{:S(2)}) copy-start(bf16[48,32]{0,1:T(8,128)(2,1)} %param.7) | copy-start | bytes 9220
  6.5 122.6 %all-gather.2.cloned.1.call-start = ((), (), s32[]{:S(2)}) async-start(), calls=%async_computation.4 | async-start | bytes 6684672 | tf_op jit(solution)/shard_map/all_gather | solution.py:47
  8.8 18.0 %all-to-all-start.2 = ((bf16[16,2,192]{2,1,0:T(2,128)(2,1)}), bf16[16,2,192]{2,1,0:T(2,128)(2,1)S(1)}, u32[]{:S(2)}, u32[]{:S(2)}) async-start(bf16[16,2,192]{2,1,0:T(2,128)(2,1)} %reshape.126), calls=%async_computation.2 | async-start | bytes 32768 | tf_op jit(solution)/shard_map/all_to_all | solution.py:44
  26.8 12.2 %all-to-all-start = ((bf16[16,2,768]{2,1,0:T(2,128)(2,1)}), bf16[16,2,768]{2,1,0:T(2,128)(2,1)S(1)}, u32[]{:S(2)}, u32[]{:S(2)}) async-start(bf16[16,2,768]{2,1,0:T(2,128)(2,1)} %reshape.124), calls=%async_computation | async-start | bytes 98304 | tf_op jit(solution)/shard_map/all_to_all | solution.py:49
  39.0 4.5 %copy-start.4 = (bf16[16,2,768]{2,1,0:T(2,128)(2,1)}, bf16[16,2,768]{2,1,0:T(2,128)(2,1)S(1)}, u32[]{:S(2)}) copy-start(bf16[16,2,768]{2,1,0:T(2,128)(2,1)S(1)} %all-to-all-done) | copy-start | bytes 147460
  39.0 59.8 %all-to-all-start.1 = ((bf16[48,16,1024]{2,0,1:T(8,128)(2,1)}), bf16[48,16,1024]{2,0,1:T(8,128)(2,1)}, u32[]{:S(2)}, u32[]{:S(2)}) async-start(bf16[48,16,1024]{2,0,1:T(8,128)(2,1)} %bitcast.69), calls=%async_computation.1 | async-start | bytes 3145728 | tf_op jit(solution)/shard_map/all_to_all | solution.py:43
  43.4 281.4 %reduce-scatter.2.cloned.1.call-start = ((), (), s32[]{:S(2)}) async-start(), calls=%async_computation.5 | async-start | bytes 8912896 | tf_op jit(solution)/shard_map/reduce_scatter | solution.py:54
  55.1 45.5 %copy-start.3 = (f32[6,128,1024]{2,1,0:T(8,128)S(1)}, f32[6,128,1024]{2,1,0:T(8,128)}, u32[]{:S(2)}) copy-start(f32[6,128,1024]{2,1,0:T(8,128)} %mul.152) | copy-start | bytes 9437188
  145.2 32.4 %copy-start.2 = (bf16[6,128,4096]{2,1,0:T(8,128)(2,1)}, bf16[6,128,4096]{2,1,0:T(8,128)(2,1)S(1)}, u32[]{:S(2)}) copy-start(bf16[6,128,4096]{2,1,0:T(8,128)(2,1)S(1)} %divide_convert_fusion) | copy-start | bytes 18874372
  185.9 138.9 %copy-start.1 = (bf16[48,32]{0,1:T(8,128)(2,1)S(1)}, bf16[48,32]{0,1:T(8,128)(2,1)}, u32[]{:S(2)}) copy-start(bf16[48,32]{0,1:T(8,128)(2,1)} %param.7) | copy-start | bytes 9220
Sparse Core Ops, SparseCore 0:
  9.1 119.9 all-gather.1
  218.3 106.4 reduce-scatter.1
